TPU v7x, 32 devices: a whole 2x2x4 slice. The times are simulated.
32 devices in a mesh: angle: 8 (over y, x, core), scan: 4 (over z).
Axes of the slice: x: 2, y: 2, z: 4, core: 2. Of those that a mesh axis runs over, the one named last changes fastest.
Arguments:
- object_slices: float32 [2, 3, 256, 512], P(None, None, 'scan', 'angle'), may hold values from -5 to 5
- probe: float32 [2, 128, 128], replicated, may hold values from -6 to 6
- intensities: float32 [8, 4, 2, 128, 128], P('angle', 'scan'), may hold values from 0.5 to 3.5
- row_offsets: int32 [8, 4, 2], P('angle', 'scan'), may hold values from 0 to 64
- column_starts: int32 [8, 4, 2], P('angle', 'scan'), may hold values from 0 to 320
- slice_shifts: int32 [8, 3], P('angle'), may hold values from 0 to 64
- counts: int32 [8, 4], P('angle', 'scan'), may hold values from 1 to 2, as said below
Outputs:
- object_gradient: float32 [2, 3, 256, 512], P(None, None, 'scan', 'angle')
- probe_gradient: float32 [2, 128, 128], replicated
Inputs may be any that keep to these rules, and one draw needn't show every extreme that they name: `counts`: the largest value 2 occurs in every draw.
All inputs are finite; a program needn't handle non-finite values.
Results may differ from a plain program's by a relative error of at most 0.0003.
Values sent between devices are 32-bit elements; how exact they have to be, the bound alone decides.
A program may use at most 64 MiB of HBM per device.

v0:
```python
from functools import partial
import jax
import jax.numpy as jnp
from jax import lax
from jax.sharding import PartitionSpec as P


def padded(cells, sides, width):
    for axis, dim in sides:
        count = lax.axis_size(axis)
        ends = count - 1
        head = lax.slice_in_dim(cells, 0, width, axis=dim)
        tail = lax.slice_in_dim(cells, cells.shape[dim] - width, cells.shape[dim], axis=dim)
        cells = jnp.concatenate(
            [
                lax.ppermute(tail, axis, [(i, (i + 1) % count) for i in range(ends)]),
                cells,
                lax.ppermute(head, axis, [((i + 1) % count, i) for i in range(ends)]),
            ],
            axis=dim,
        )
    return cells


def propagator(size):
    index = jnp.arange(size, dtype=jnp.int32)
    centred = ((index + size // 2) % size - size // 2).astype(jnp.float32)
    radius = centred[:, None] * centred[:, None] + centred[None, :] * centred[None, :]
    phase = 8.0 * jnp.pi * radius / (size * size)
    return (jnp.cos(phase), jnp.sin(phase))


def tables(size):
    index = jnp.arange(size, dtype=jnp.int32)
    turns = index[:, None] * index[None, :] % size
    phase = 2.0 * jnp.pi * turns.astype(jnp.float32) / size
    scale = 1.0 / jnp.sqrt(jnp.float32(size))
    return (jnp.cos(phase) * scale, jnp.sin(phase) * scale)


def matmul(first, second):
    return jnp.dot(
        first, second, precision=lax.Precision.HIGHEST, preferred_element_type=jnp.float32
    )


def transform(real_part, imag_part, cosine, sine, sign):
    left_re = matmul(cosine, real_part) - sign * matmul(sine, imag_part)
    left_im = matmul(cosine, imag_part) + sign * matmul(sine, real_part)
    right_re = matmul(left_re, cosine) - sign * matmul(left_im, sine)
    right_im = matmul(left_im, cosine) + sign * matmul(left_re, sine)
    return (right_re, right_im)


def local_loss(slab, probe, measured, weight, cosine, sine, kern_re, kern_im):
    wave_re, wave_im = (probe[0], probe[1])
    layers = slab.shape[1]
    for k in range(layers):
        object_re, object_im = (slab[0, k], slab[1, k])
        wave_re, wave_im = (
            wave_re * object_re - wave_im * object_im,
            wave_re * object_im + wave_im * object_re,
        )
        if k + 1 < layers:
            freq_re, freq_im = transform(wave_re, wave_im, cosine, sine, -1.0)
            freq_re, freq_im = (
                freq_re * kern_re - freq_im * kern_im,
                freq_re * kern_im + freq_im * kern_re,
            )
            wave_re, wave_im = transform(freq_re, freq_im, cosine, sine, 1.0)
    far_re, far_im = transform(wave_re, wave_im, cosine, sine, -1.0)
    differ = far_re * far_re + far_im * far_im - measured
    return weight * jnp.sum(differ * differ)


def local(object_slices, probe, intensities, row_offsets, column_starts, slice_shifts, counts):
    band = object_slices.shape[2]
    framed = padded(object_slices, (("scan", 2),), band)
    region = lax.all_gather(framed, "angle", axis=3, tiled=True)
    size = probe.shape[1]
    slots = row_offsets.shape[2]
    layers = region.shape[1]
    angles = lax.axis_size("angle")
    cosine, sine = tables(size)
    kern_re, kern_im = propagator(size)
    shifts = slice_shifts[0]
    zero = jnp.zeros((), jnp.int32)

    def visit(slot, carry):
        gradient_region, gradient_probe = carry
        top = row_offsets[0, 0, slot]
        start = column_starts[0, 0, slot]
        slab = jnp.concatenate(
            [
                lax.dynamic_slice(
                    region, (zero, zero + k, top, start + shifts[k]), (2, 1, size, size)
                )
                for k in range(layers)
            ],
            axis=1,
        )
        weight = jnp.where(slot < counts[0, 0], 0.5 / angles, 0.0).astype(jnp.float32)
        measured = intensities[0, 0, slot]
        scorer = partial(
            local_loss,
            measured=measured,
            weight=weight,
            cosine=cosine,
            sine=sine,
            kern_re=kern_re,
            kern_im=kern_im,
        )
        loss, pull = jax.vjp(scorer, slab, probe)
        slab_grad, probe_grad = pull(jnp.ones_like(loss))
        for k in range(layers):
            place = (zero, zero + k, top, start + shifts[k])
            current = lax.dynamic_slice(gradient_region, place, (2, 1, size, size))
            gradient_region = lax.dynamic_update_slice(
                gradient_region, current + slab_grad[:, k : k + 1], place
            )
        return (gradient_region, gradient_probe + probe_grad)

    start_carry = (jnp.zeros(region.shape, jnp.float32), jnp.zeros(probe.shape, jnp.float32))
    gradient_region, gradient_probe = lax.fori_loop(0, slots, visit, start_carry)
    shared = lax.psum_scatter(gradient_region, "angle", scatter_dimension=3, tiled=True)
    edges = jnp.concatenate([shared[:, :, :band], shared[:, :, 2 * band :]], axis=2)
    rimmed = padded(edges, (("scan", 2),), band)
    object_gradient = shared[:, :, band : 2 * band] + rimmed[:, :, :band] + rimmed[:, :, 3 * band :]
    group_total = lax.psum(gradient_probe, "scan")
    probe_gradient = lax.psum(group_total, "angle")
    return (object_gradient, probe_gradient)


def solution(mesh):
    return jax.shard_map(
        local,
        mesh=mesh,
        in_specs=(
            P(None, None, "scan", "angle"),
            P(),
            P("angle", "scan", None, None, None),
            P("angle", "scan", None),
            P("angle", "scan", None),
            P("angle", None),
            P("angle", "scan"),
        ),
        out_specs=(P(None, None, "scan", "angle"), P()),
        check_vma=False,
    )
```

profile of v0, /device:TPU:0, one launch (start us, length us, event | category | flops | bytes accessed | tf_op | source)
XLA Modules:
  0.0 352.9 jit_solution(17662193562692884179)
XLA Ops:
  8.3 1.3 collective-permute-start.1
  9.6 5.6 %collective-permute-start = (f32[2,3,64,64]{2,0,1,3:T(2,128)S(1)}, f32[2,3,64,64]{2,0,1,3:T(2,128)S(1)}, u32[]{:S(2)}, u32[]{:S(2)}) collective-permute-start(f32[2,3,64,64]{2,0,1,3:T(2,128)S(1)} %copy.25), channel_id=1, source_target_pairs={{0,1},{1,2},{2,3},{4,5},{5,6},{6,7},{8,9},{9,10},{10,11},{12,13},{... | collective-permute-start | bytes 294920 | tf_op jit(solution)/shard_map/ppermute | solution.py:16
  15.2 2.9 collective-permute-done.1
  20.7 34.6 %all-gather.2.cloned.1.call-done = f32[2,3,192,512]{2,0,1,3:T(2,128)} async-done(((f32[2,3,192,64]{2,0,1,3:T(2,128)}), f32[2,3,192,512]{2,0,1,3:T(2,128)}) %all-gather.2.cloned.1.call-update) | async-done | bytes 2359312 | tf_op jit(solution)/shard_map/all_gather | solution.py:79
  55.2 5.6 %copy.28 = f32[2,3,192,512]{3,2,1,0:T(8,128)} copy(f32[2,3,192,512]{2,0,1,3:T(2,128)} %all-gather.2.cloned.1.call-done) | data formatting | bytes 4718592
  61.8 137.1 %while.19 = (s32[]{:T(128)}, f32[2,3,192,512]{3,2,1,0:T(8,128)S(1)}, f32[2,128,128]{2,1,0:T(8,128)S(1)}, s32[1,1,2]{2,1,0:T(1,128)S(1)}, s32[1,1,2]{2,1,0:T(1,12...) while((s32[]{:T(128)}, ...), condition=%wide.region_1.2_spmd.clone.clone.clone.clone, body=%wide.region_0.1_spmd.clone.clone.clone.clone.sunk | while | flops 2037301248 | bytes 20128300 | solution.py:124
  79.3 1.5 multiply_add_fusion.7
  85.5 1.3 convolution_add_fusion.37
  89.9 1.5 multiply_subtract_fusion.3
  99.0 1.5 add_bitcast_fusion.9
  109.5 1.5 add_bitcast_fusion.10
  120.1 1.5 add_bitcast_fusion.11
  121.8 2.3 dynamic_update_slice.36
  124.3 2.3 dynamic_update_slice.37
  126.7 2.3 dynamic_update_slice.38
  146.8 1.5 multiply_add_fusion.7
  157.0 1.5 multiply_subtract_fusion.3
  166.1 1.5 add_bitcast_fusion.9
  176.7 1.5 add_bitcast_fusion.10
  187.4 1.5 add_bitcast_fusion.11
  189.2 2.3 dynamic_update_slice.36
  191.6 2.3 dynamic_update_slice.37
  194.0 2.3 dynamic_update_slice.38
  199.0 3.4 copy.37
  202.4 6.0 %reshape.42 = f32[512,1152]{1,0:T(8,128)} reshape(f32[512,2,3,192]{3,2,1,0:T(4,128)} %bitcast.367) | data formatting | bytes 4718592
  209.2 41.8 %reduce-scatter.4.cloned.1.call-done = f32[64,1152]{1,0:T(8,128)} async-done(((f32[512,1152]{1,0:T(8,128)}), f32[64,1152]{1,0:T(8,128)}) %reduce-scatter.4.cloned.1.call-update) | async-done | bytes 294928
  250.9 1.3 reshape.43
  252.8 1.3 collective-permute-start.3
  254.1 4.6 %collective-permute-start.2 = (f32[2,3,64,64]{3,2,1,0:T(8,128)S(1)}, f32[2,3,64,64]{3,2,1,0:T(8,128)S(1)}, u32[]{:S(2)}, u32[]{:S(2)}) collective-permute-start(f32[2,3,64,64]{3,2,1,0:T(8,128)S(1)} %copy.40), channel_id=1, source_target_pairs={{0,1},{1,2},{2,3},{4,5},{5,6},{6,7},{8,9},{9,10},{10,11},{12,13},{... | collective-permute-start | bytes 294920 | tf_op jit(solution)/shard_map/ppermute | solution.py:16
  258.6 29.9 %all-reduce.11.cloned.1.call-done = f32[2,128,128]{2,1,0:T(8,128)} async-done(((f32[2,128,128]{2,1,0:T(8,128)}), f32[2,128,128]{2,1,0:T(8,128)}) %all-reduce.11.cloned.1.call-update) | async-done | bytes 131088 | tf_op jit(solution)/shard_map/psum | solution.py:129
  289.4 55.2 %all-reduce.13.cloned.1.call-done = f32[2,128,128]{2,1,0:T(8,128)} async-done(((f32[2,128,128]{2,1,0:T(8,128)}), f32[2,128,128]{2,1,0:T(8,128)}) %all-reduce.13.cloned.1.call-update) | async-done | bytes 131088 | tf_op jit(solution)/shard_map/psum | solution.py:130
  344.6 1.6 copy.56
  (198 shorter events, 96.8 us)
Async XLA Ops:
  7.2 48.1 %all-gather.2.cloned.1.call-start = ((), (), s32[]{:S(2)}) async-start(), calls=%async_computation.1 | async-start | bytes 3538944 | tf_op jit(solution)/shard_map/all_gather | solution.py:79
  8.3 9.9 %collective-permute-start.1 = (f32[2,3,64,64]{2,0,1,3:T(2,128)S(1)}, f32[2,3,64,64]{2,0,1,3:T(2,128)S(1)}, u32[]{:S(2)}, u32[]{:S(2)}) collective-permute-start(f32[2,3,64,64]{2,0,1,3:T(2,128)S(1)} %copy.25), channel_id=1, source_target_pairs={{1,0},{2,1},{3,2},{5,4},{6,5},{7,6},{9,8},{10,9},{11,10},{13,12},{... | collective-permute-start | bytes 294920 | tf_op jit(solution)/shard_map/ppermute | solution.py:18
  9.6 9.7 %collective-permute-start = (f32[2,3,64,64]{2,0,1,3:T(2,128)S(1)}, f32[2,3,64,64]{2,0,1,3:T(2,128)S(1)}, u32[]{:S(2)}, u32[]{:S(2)}) collective-permute-start(f32[2,3,64,64]{2,0,1,3:T(2,128)S(1)} %copy.25), channel_id=1, source_target_pairs={{0,1},{1,2},{2,3},{4,5},{5,6},{6,7},{8,9},{9,10},{10,11},{12,13},{... | collective-permute-start | bytes 294920 | tf_op jit(solution)/shard_map/ppermute | solution.py:16
  20.6 230.3 %reduce-scatter.4.cloned.1.call-start = ((), (), s32[]{:S(2)}) async-start(), calls=%async_computation.4 | async-start | bytes 2654208
  60.8 0.9 copy-start
  60.8 0.9 copy-start.2
  60.8 0.9 copy-start.3
  60.8 0.9 copy-start.4
  60.8 1.0 copy-start.5
  199.0 3.4 copy-start.1
  208.4 80.1 %all-reduce.11.cloned.1.call-start = ((), (), s32[]{:S(2)}) async-start(), calls=%async_computation.2 | async-start | bytes 262144 | tf_op jit(solution)/shard_map/psum | solution.py:129
  209.1 135.5 %all-reduce.13.cloned.1.call-start = ((), (), s32[]{:S(2)}) async-start(), calls=%async_computation.3 | async-start | bytes 262144 | tf_op jit(solution)/shard_map/psum | solution.py:130
  252.8 35.9 %collective-permute-start.3 = (f32[2,3,64,64]{3,2,1,0:T(8,128)S(1)}, f32[2,3,64,64]{3,2,1,0:T(8,128)S(1)}, u32[]{:S(2)}, u32[]{:S(2)}) collective-permute-start(f32[2,3,64,64]{3,2,1,0:T(8,128)S(1)} %copy.41), channel_id=1, source_target_pairs={{1,0},{2,1},{3,2},{5,4},{6,5},{7,6},{9,8},{10,9},{11,10},{13,12},{... | collective-permute-start | bytes 294920 | tf_op jit(solution)/shard_map/ppermute | solution.py:18
  254.1 34.6 %collective-permute-start.2 = (f32[2,3,64,64]{3,2,1,0:T(8,128)S(1)}, f32[2,3,64,64]{3,2,1,0:T(8,128)S(1)}, u32[]{:S(2)}, u32[]{:S(2)}) collective-permute-start(f32[2,3,64,64]{3,2,1,0:T(8,128)S(1)} %copy.40), channel_id=1, source_target_pairs={{0,1},{1,2},{2,3},{4,5},{5,6},{6,7},{8,9},{9,10},{10,11},{12,13},{... | collective-permute-start | bytes 294920 | tf_op jit(solution)/shard_map/ppermute | solution.py:16
Sparse Core Ops, SparseCore 0:
  20.7 34.4 all-gather.1
  208.5 42.3 reduce-scatter.3
  253.8 34.6 all-reduce.10
  291.4 53.1 all-reduce.12
where the time goes:
time: 356 us; the launch traced here: 353 us
  waiting for transfers between devices  166 us (47%)
  matrix products  101 us (28%)
  local copies, waits for them, and re-layouts  36.8 us (10%)
  loops' own time  16.9 us (5%)
  between operations  14.1 us (4%)
  starting transfers between devices  12.9 us (4%)
  other arithmetic  4.94 us (1%)
    dot_general x160, matrix products, matmul(): jnp.dot(first, second, precision=lax.Precision.HIGHEST, preferred_element...  101 us
    psum x1, waiting for transfers between devices, local(): probe_gradient = lax.psum(group_total, 'angle')  55.2 us
    unnamed x5, waiting for transfers between devices  42.5 us
    all_gather x1, waiting for transfers between devices, local(): region = lax.all_gather(framed, 'angle', axis=3, tiled=True)  34.6 us
    psum x1, waiting for transfers between devices, local(): group_total = lax.psum(gradient_probe, 'scan')  29.9 us
    unnamed x21, local copies, waits for them, and re-layouts  20 us
    another operation x1, loops' own time, local(): lax.fori_loop(0, slots, visit, start_carry)  16.9 us
    dynamic_update_slice x6, local copies, waits for them, and re-layouts, visit(): lax.dynamic_update_slice(gradient_region, current + slab_grad[:, k:k + 1]...  13.8 us
  transfers between devices with their start and end apart: 8, of which 6 were waited for; matrix products, arithmetic and copies ran while one was open for 1% of the time, Pallas kernels for 0%

commit v1 on v0

--- a/solution.py
+++ b/solution.py
@@ -126,7 +126,7 @@
     edges = jnp.concatenate([shared[:, :, :band], shared[:, :, 2 * band :]], axis=2)
     rimmed = padded(edges, (("scan", 2),), band)
     object_gradient = shared[:, :, band : 2 * band] + rimmed[:, :, :band] + rimmed[:, :, 3 * band :]
-    group_total = lax.psum(gradient_probe, "scan")
+    group_total = jnp.sum(lax.all_gather(gradient_probe, "scan"), axis=0)
     probe_gradient = lax.psum(group_total, "angle")
     return (object_gradient, probe_gradient)
 

time: 356 us -> 341 us (0.958)
  waiting for transfers between devices: 166 us -> 134 us
  blocking collectives: 0 us -> 16.9 us
    psum x1 -> x0, waiting for transfers between devices: 29.9 us -> none  [local(): group_total = lax.psum(gradient_probe, 'scan')]
    all_gather x0 -> x1, blocking collectives: none -> 16.9 us  [local(): group_total = jnp.sum(lax.all_gather(gradient_probe, 'scan'), axis=0)]
    unnamed x5 -> x4, waiting for transfers between devices: 42.5 us -> 42.6 us
    unnamed x21 -> x19, local copies, waits for them, and re-layouts: 20 us -> 20 us
  transfers between devices with their start and end apart: 8 -> 7, of which waited for: 6 -> 5; matrix products, arithmetic and copies ran while one was open for 1% -> 0% of each run, Pallas kernels for 0% -> 0%
where the time goes in v1:
time: 341 us; the launch traced here: 338 us
  waiting for transfers between devices  134 us (39%)
  matrix products  101 us (30%)
  local copies, waits for them, and re-layouts  36.7 us (11%)
  blocking collectives  16.9 us (5%)
  loops' own time  16.4 us (5%)
  between operations  14.1 us (4%)
  starting transfers between devices  12.9 us (4%)
  other arithmetic  5.66 us (2%)
    dot_general x160, matrix products, matmul(): jnp.dot(first, second, precision=lax.Precision.HIGHEST, preferred_element...  101 us
    psum x1, waiting for transfers between devices, local(): probe_gradient = lax.psum(group_total, 'angle')  53.2 us
    unnamed x4, waiting for transfers between devices  42.6 us
    all_gather x1, waiting for transfers between devices, local(): region = lax.all_gather(framed, 'angle', axis=3, tiled=True)  34.6 us
    unnamed x19, local copies, waits for them, and re-layouts  20 us
    all_gather x1, blocking collectives, local(): group_total = jnp.sum(lax.all_gather(gradient_probe, 'scan'), axis=0)  16.9 us
    another operation x1, loops' own time, local(): lax.fori_loop(0, slots, visit, start_carry)  16.4 us
    dynamic_update_slice x6, local copies, waits for them, and re-layouts, visit(): lax.dynamic_update_slice(gradient_region, current + slab_grad[:, k:k + 1]...  13.8 us
  transfers between devices with their start and end apart: 7, of which 5 were waited for; matrix products, arithmetic and copies ran while one was open for 0% of the time, Pallas kernels for 0%

profile of v1, /device:TPU:0, one launch (start us, length us, event | category | flops | bytes accessed | tf_op | source)
XLA Modules:
  0.0 338.0 jit_solution(12044905494210382741)
XLA Ops:
  8.3 1.3 collective-permute-start.1
  9.6 5.6 %collective-permute-start = (f32[2,3,64,64]{2,0,1,3:T(2,128)S(1)}, f32[2,3,64,64]{2,0,1,3:T(2,128)S(1)}, u32[]{:S(2)}, u32[]{:S(2)}) collective-permute-start(f32[2,3,64,64]{2,0,1,3:T(2,128)S(1)} %copy.25), channel_id=1, source_target_pairs={{0,1},{1,2},{2,3},{4,5},{5,6},{6,7},{8,9},{9,10},{10,11},{12,13},{... | collective-permute-start | bytes 294920 | tf_op jit(solution)/shard_map/ppermute | solution.py:16
  15.2 2.9 collective-permute-done.1
  20.7 34.6 %all-gather.3.cloned.1.call-done = f32[2,3,192,512]{2,0,1,3:T(2,128)} async-done(((f32[2,3,192,64]{2,0,1,3:T(2,128)}), f32[2,3,192,512]{2,0,1,3:T(2,128)}) %all-gather.3.cloned.1.call-update) | async-done | bytes 2359312 | tf_op jit(solution)/shard_map/all_gather | solution.py:79
  55.3 5.5 %copy.28 = f32[2,3,192,512]{3,2,1,0:T(8,128)} copy(f32[2,3,192,512]{2,0,1,3:T(2,128)} %all-gather.3.cloned.1.call-done) | data formatting | bytes 4718592
  61.8 136.5 %while.19 = (s32[]{:T(128)}, f32[2,3,192,512]{3,2,1,0:T(8,128)S(1)}, f32[2,128,128]{2,1,0:T(8,128)S(1)}, s32[1,1,2]{2,1,0:T(1,128)S(1)}, s32[1,1,2]{2,1,0:T(1,12...) while((s32[]{:T(128)}, ...), condition=%wide.region_1.2_spmd.clone.clone.clone.clone, body=%wide.region_0.1_spmd.clone.clone.clone.clone.sunk | while | flops 2037301248 | bytes 20128300 | solution.py:124
  79.0 1.5 multiply_add_fusion.7
  85.2 1.3 convolution_add_fusion.37
  89.6 1.5 multiply_subtract_fusion.3
  98.6 1.5 add_bitcast_fusion.9
  109.2 1.5 add_bitcast_fusion.10
  119.8 1.5 add_bitcast_fusion.11
  121.5 2.3 dynamic_update_slice.36
  123.9 2.3 dynamic_update_slice.37
  126.4 2.3 dynamic_update_slice.38
  146.1 1.5 multiply_add_fusion.7
  156.4 1.5 multiply_subtract_fusion.3
  165.4 1.5 add_bitcast_fusion.9
  176.0 1.5 add_bitcast_fusion.10
  186.8 1.5 add_bitcast_fusion.11
  188.5 2.3 dynamic_update_slice.36
  190.9 2.3 dynamic_update_slice.37
  193.3 2.3 dynamic_update_slice.38
  198.3 3.4 %copy.37 = f32[2,3,192,512]{2,1,0,3:T(4,128)} copy(f32[2,3,192,512]{3,2,1,0:T(8,128)S(1)} %get-tuple-element.508) | data formatting | bytes 4718592
  201.8 6.0 %reshape.43 = f32[512,1152]{1,0:T(8,128)} reshape(f32[512,2,3,192]{3,2,1,0:T(4,128)} %bitcast.368) | data formatting | bytes 4718592
  207.8 42.5 %reduce-scatter.4.cloned.1.call-done = f32[64,1152]{1,0:T(8,128)} async-done(((f32[512,1152]{1,0:T(8,128)}), f32[64,1152]{1,0:T(8,128)}) %reduce-scatter.4.cloned.1.call-update) | async-done | bytes 294928
  250.3 1.3 reshape.44
  252.2 1.3 collective-permute-start.3
  253.5 4.6 %collective-permute-start.2 = (f32[2,3,64,64]{3,2,1,0:T(8,128)S(1)}, f32[2,3,64,64]{3,2,1,0:T(8,128)S(1)}, u32[]{:S(2)}, u32[]{:S(2)}) collective-permute-start(f32[2,3,64,64]{3,2,1,0:T(8,128)S(1)} %copy.40), channel_id=1, source_target_pairs={{0,1},{1,2},{2,3},{4,5},{5,6},{6,7},{8,9},{9,10},{10,11},{12,13},{... | collective-permute-start | bytes 294920 | tf_op jit(solution)/shard_map/ppermute | solution.py:16
  258.0 16.9 %all-gather = f32[8,128,128]{2,1,0:T(8,128)S(1)} all-gather(f32[2,128,128]{2,1,0:T(8,128)S(1)} %get-tuple-element.509), channel_id=2, replica_groups=mesh['angle'=8,'scan'=4] {'scan'}, dimensions={0}, use_global_device_ids=true | all-gather | bytes 655360 | tf_op jit(solution)/shard_map/all_gather | solution.py:129
  276.5 53.2 %all-reduce.10.cloned.1.call-done = f32[2,128,128]{2,1,0:T(8,128)} async-done(((f32[2,128,128]{2,1,0:T(8,128)}), f32[2,128,128]{2,1,0:T(8,128)}) %all-reduce.10.cloned.1.call-update) | async-done | bytes 131088 | tf_op jit(solution)/shard_map/psum | solution.py:130
  329.7 1.6 copy.55
  (195 shorter events, 96.7 us)
Async XLA Ops:
  7.2 48.1 %all-gather.3.cloned.1.call-start = ((), (), s32[]{:S(2)}) async-start(), calls=%async_computation.1 | async-start | bytes 3538944 | tf_op jit(solution)/shard_map/all_gather | solution.py:79
  8.3 9.9 %collective-permute-start.1 = (f32[2,3,64,64]{2,0,1,3:T(2,128)S(1)}, f32[2,3,64,64]{2,0,1,3:T(2,128)S(1)}, u32[]{:S(2)}, u32[]{:S(2)}) collective-permute-start(f32[2,3,64,64]{2,0,1,3:T(2,128)S(1)} %copy.25), channel_id=1, source_target_pairs={{1,0},{2,1},{3,2},{5,4},{6,5},{7,6},{9,8},{10,9},{11,10},{13,12},{... | collective-permute-start | bytes 294920 | tf_op jit(solution)/shard_map/ppermute | solution.py:18
  9.6 9.7 %collective-permute-start = (f32[2,3,64,64]{2,0,1,3:T(2,128)S(1)}, f32[2,3,64,64]{2,0,1,3:T(2,128)S(1)}, u32[]{:S(2)}, u32[]{:S(2)}) collective-permute-start(f32[2,3,64,64]{2,0,1,3:T(2,128)S(1)} %copy.25), channel_id=1, source_target_pairs={{0,1},{1,2},{2,3},{4,5},{5,6},{6,7},{8,9},{9,10},{10,11},{12,13},{... | collective-permute-start | bytes 294920 | tf_op jit(solution)/shard_map/ppermute | solution.py:16
  20.6 229.7 %reduce-scatter.4.cloned.1.call-start = ((), (), s32[]{:S(2)}) async-start(), calls=%async_computation.3 | async-start | bytes 2654208
  60.8 0.9 copy-start
  60.8 0.9 copy-start.1
  60.8 0.9 copy-start.2
  60.8 0.9 copy-start.3
  60.8 1.0 copy-start.4
  207.8 121.9 %all-reduce.10.cloned.1.call-start = ((), (), s32[]{:S(2)}) async-start(), calls=%async_computation.2 | async-start | bytes 262144 | tf_op jit(solution)/shard_map/psum | solution.py:130
  252.2 23.6 %collective-permute-start.3 = (f32[2,3,64,64]{3,2,1,0:T(8,128)S(1)}, f32[2,3,64,64]{3,2,1,0:T(8,128)S(1)}, u32[]{:S(2)}, u32[]{:S(2)}) collective-permute-start(f32[2,3,64,64]{3,2,1,0:T(8,128)S(1)} %copy.41), channel_id=1, source_target_pairs={{1,0},{2,1},{3,2},{5,4},{6,5},{7,6},{9,8},{10,9},{11,10},{13,12},{... | collective-permute-start | bytes 294920 | tf_op jit(solution)/shard_map/ppermute | solution.py:18
  253.5 22.3 %collective-permute-start.2 = (f32[2,3,64,64]{3,2,1,0:T(8,128)S(1)}, f32[2,3,64,64]{3,2,1,0:T(8,128)S(1)}, u32[]{:S(2)}, u32[]{:S(2)}) collective-permute-start(f32[2,3,64,64]{3,2,1,0:T(8,128)S(1)} %copy.40), channel_id=1, source_target_pairs={{0,1},{1,2},{2,3},{4,5},{5,6},{6,7},{8,9},{9,10},{10,11},{12,13},{... | collective-permute-start | bytes 294920 | tf_op jit(solution)/shard_map/ppermute | solution.py:16
Sparse Core Ops, SparseCore 0:
  20.7 34.4 all-gather.2
  207.9 42.3 reduce-scatter.3
  275.7 53.8 all-reduce.9
